TPU v7x, 32 devices: a whole 2x2x4 slice. The times are simulated.
32 devices in a mesh: fsdp: 4 (over y, x), tp: 8 (over z, core).
Axes of the slice: x: 2, y: 2, z: 4, core: 2. Of those that a mesh axis runs over, the one named last changes fastest.
Arguments:
- tokens: bfloat16 [1024, 8192], P('fsdp', 'tp'), may hold values from -6 to 6
- out_grad: bfloat16 [1024, 8192], P('fsdp', 'tp'), may hold values from -6 to 6
- gate_weight: bfloat16 [8192, 1024], P('fsdp', 'tp'), may hold values from -0.0625 to 0.0625
- up_weight: bfloat16 [8192, 1024], P('fsdp', 'tp'), may hold values from -0.0625 to 0.0625
- down_weight: bfloat16 [1024, 8192], P('tp', 'fsdp'), may hold values from -0.1875 to 0.1875
Outputs:
- input_grad: bfloat16 [1024, 8192], P('fsdp', 'tp')
- gate_grad: float32 [8192, 1024], P('fsdp', 'tp')
- up_grad: float32 [8192, 1024], P('fsdp', 'tp')
- down_grad: float32 [1024, 8192], P('tp', 'fsdp')
All inputs are finite; a program needn't handle non-finite values.
Results may differ from a plain program's by a relative error of at most 0.0023.
Values may be sent and summed in bfloat16 or wider, within the bound.
A program may use at most 128 MiB of HBM per device.

v0:
```python
import math

import jax
import jax.numpy as jnp
from jax import lax
from jax.sharding import PartitionSpec as P


def over_all(shard, axis, dim, absorb, state):
    everything = jax.tree.map(lambda a: lax.all_gather(a, axis, axis=dim, tiled=True), shard)
    return absorb(state, everything, jnp.int32(0))


def own_rows(portion, rows, axis):
    count = rows * lax.axis_size(axis)
    return lax.psum_scatter(portion(jnp.int32(0), count), axis, scatter_dimension=0, tiled=True)


def column_term(left, right, start, count, factor):
    block = lax.dynamic_slice_in_dim(left, start, count, 1)
    product = lax.dot_general(
        block, right, (((0,), (0,)), ((), ())), preferred_element_type=jnp.float32
    )
    return product * factor


def body(tokens, out_grad, gate_weight, up_weight, down_weight):
    factor = 1.0 / math.sqrt(tokens.shape[0] * lax.axis_size("fsdp"))
    whole = lax.all_gather(tokens, "tp", axis=1, tiled=True)
    grads = lax.all_gather(out_grad, "tp", axis=1, tiled=True)
    gate_full, up_full = (
        lax.all_gather(gate_weight, "fsdp", axis=0, tiled=True),
        lax.all_gather(up_weight, "fsdp", axis=0, tiled=True),
    )
    gate = jnp.dot(whole, gate_full, preferred_element_type=jnp.float32)
    up = jnp.dot(whole, up_full, preferred_element_type=jnp.float32)

    def add_down(total, piece, start):
        columns = lax.dynamic_slice_in_dim(grads, start, piece.shape[1], 1)
        return total + lax.dot_general(
            columns, piece, (((1,), (1,)), ((), ())), preferred_element_type=jnp.float32
        )

    initial = jnp.zeros((whole.shape[0], down_weight.shape[0]), jnp.float32)
    hidden_grad = over_all(down_weight, "fsdp", 1, add_down, initial)
    squashed = jax.nn.sigmoid(gate)
    activated = gate * squashed
    slope = squashed * (1.0 + gate * (1.0 - squashed))
    hidden = (activated * up).astype(jnp.bfloat16)
    gate_delta = (hidden_grad * up * slope).astype(jnp.bfloat16)
    up_delta = (hidden_grad * activated).astype(jnp.bfloat16)
    partial_term = jnp.dot(gate_delta, gate_full.T, preferred_element_type=jnp.float32)
    partial_term = partial_term + jnp.dot(up_delta, up_full.T, preferred_element_type=jnp.float32)
    input_grad = lax.psum_scatter(partial_term, "tp", scatter_dimension=1, tiled=True).astype(
        jnp.bfloat16
    )
    rows_here = gate_weight.shape[0]

    def joint_term(start, count):
        return jnp.concatenate(
            [
                column_term(whole, gate_delta, start, count, factor),
                column_term(whole, up_delta, start, count, factor),
                column_term(grads, hidden, start, count, factor),
            ],
            axis=1,
        )

    summed = own_rows(joint_term, rows_here, "fsdp")
    width = gate_delta.shape[1]
    gate_grad = summed[:, :width]
    up_grad = summed[:, width : 2 * width]
    down_grad = summed[:, 2 * width :].T
    return (input_grad, gate_grad, up_grad, down_grad)


def solution(mesh):
    return jax.shard_map(
        body,
        mesh=mesh,
        in_specs=(
            P("fsdp", "tp"),
            P("fsdp", "tp"),
            P("fsdp", "tp"),
            P("fsdp", "tp"),
            P("tp", "fsdp"),
        ),
        out_specs=(P("fsdp", "tp"), P("fsdp", "tp"), P("fsdp", "tp"), P("tp", "fsdp")),
        check_vma=False,
    )
```

profile of v0, /device:TPU:13, one launch (start us, length us, event | category | flops | bytes accessed | tf_op | source)
XLA Modules:
  0.0 448.3 jit_solution(9459281939705098741)
XLA Ops:
  7.2 0.0 all-gather.14.cloned.1.call-start
  7.2 0.7 all-gather.14.cloned.1.call-update
  7.9 0.0 all-gather.10.cloned.1.call-start
  7.9 0.7 all-gather.10.cloned.1.call-update
  8.6 0.0 all-gather.12.cloned.1.call-start
  8.7 0.7 all-gather.12.cloned.1.call-update
  9.4 0.0 all-gather.8.cloned.1.call-start
  9.4 0.5 all-gather.8.cloned.1.call-update
  10.0 0.0 all-gather.6.cloned.1.call-start
  10.0 0.5 all-gather.6.cloned.1.call-update
  10.5 0.0 reduce-scatter.3.cloned.1.call-start
  10.6 35.1 %all-gather.14.cloned.1.call-done = bf16[8192,128]{1,0:T(8,128)(2,1)} async-done(((bf16[2048,128]{1,0:T(8,128)(2,1)}), bf16[8192,128]{1,0:T(8,128)(2,1)}) %all-gather.14.cloned.1.call-update) | async-done | bytes 2097168 | tf_op jit(solution)/shard_map/all_gather | solution.py:32
  45.7 48.1 %all-gather.10.cloned.1.call-done = bf16[256,8192]{1,0:T(8,128)(2,1)} async-done(((bf16[256,1024]{1,0:T(8,128)(2,1)}), bf16[256,8192]{1,0:T(8,128)(2,1)}) %all-gather.10.cloned.1.call-update) | async-done | bytes 4194320 | tf_op jit(solution)/shard_map/all_gather | solution.py:29
  93.8 4.1 fusion.7
  97.9 31.9 %all-gather.12.cloned.1.call-done = bf16[8192,128]{1,0:T(8,128)(2,1)} async-done(((bf16[2048,128]{1,0:T(8,128)(2,1)}), bf16[8192,128]{1,0:T(8,128)(2,1)}) %all-gather.12.cloned.1.call-update) | async-done | bytes 2097168 | tf_op jit(solution)/shard_map/all_gather | solution.py:33
  129.9 4.1 fusion.6
  134.0 0.0 copy-start.1
  134.0 32.6 %all-gather.8.cloned.1.call-done = bf16[128,8192]{1,0:T(8,128)(2,1)} async-done(((bf16[128,2048]{1,0:T(8,128)(2,1)}), bf16[128,8192]{1,0:T(8,128)(2,1)}) %all-gather.8.cloned.1.call-update) | async-done | bytes 2097168 | tf_op jit(solution)/shard_map/all_gather | solution.py:10
  166.6 48.0 %all-gather.6.cloned.1.call-done = bf16[256,8192]{1,0:T(8,128)(2,1)} async-done(((bf16[256,1024]{1,0:T(8,128)(2,1)}), bf16[256,8192]{1,0:T(8,128)(2,1)}) %all-gather.6.cloned.1.call-update) | async-done | bytes 4194320 | tf_op jit(solution)/shard_map/all_gather | solution.py:30
  214.6 4.1 multiply_convert_fusion.1
  218.7 0.0 copy-done.1
  218.7 0.0 copy-start.2
  218.7 1.3 fusion.8
  219.9 0.3 copy-done.2
  220.3 4.5 convolution_add_fusion
  224.7 0.0 reduce-scatter.3.cloned.1.call-update
  224.8 0.0 reduce-scatter.5.cloned.1.call-start
  224.8 0.0 copy-start
  224.8 3.1 fusion.1
  227.9 0.3 copy-done
  228.3 0.0 copy-start.3
  228.3 0.8 fusion.2
  229.0 1.4 copy-done.3
  230.4 0.8 fusion
  231.3 5.0 %pad_maximum_fusion = f32[8192,384]{0,1:T(8,128)} fusion(f32[8192,128]{0,1:T(8,128)S(1)} %fusion, f32[8192,128]{0,1:T(8,128)S(1)} %fusion.1, f32[8192,128]{0,1:T(8,128)S(1)} %fusion.2), kind=kLoop, calls=%fused_computation | loop fusion | flops 6291456 | bytes 25165824 | tf_op jit(solution)/shard_map/concatenate | solution.py:60
  236.3 0.0 reduce-scatter.5.cloned.1.call-update
  236.3 76.3 %reduce-scatter.3.cloned.1.call-done = f32[256,1024]{1,0:T(8,128)} async-done(((f32[256,8192]{1,0:T(8,128)}), f32[256,1024]{1,0:T(8,128)}) %reduce-scatter.3.cloned.1.call-update) | async-done | bytes 1048592 | tf_op jit(solution)/shard_map/reduce_scatter | solution.py:54
  312.6 2.1 convert_element_type.14
  314.7 121.0 %reduce-scatter.5.cloned.1.call-done = f32[2048,384]{0,1:T(8,128)} async-done(((f32[8192,384]{0,1:T(8,128)}), f32[2048,384]{0,1:T(8,128)}) %reduce-scatter.5.cloned.1.call-update) | async-done | bytes 3145744 | tf_op jit(solution)/shard_map/reduce_scatter | solution.py:16
  435.7 3.1 slice_bitcast_fusion
  438.8 1.3 copy.9
  440.1 1.3 copy.10
Async XLA Ops:
  7.2 38.5 %all-gather.14.cloned.1.call-start = ((), (), s32[]{:S(2)}) async-start(), calls=%async_computation.6 | async-start | bytes 2621440 | tf_op jit(solution)/shard_map/all_gather | solution.py:32
  7.9 85.9 %all-gather.10.cloned.1.call-start = ((), (), s32[]{:S(2)}) async-start(), calls=%async_computation.4 | async-start | bytes 4718592 | tf_op jit(solution)/shard_map/all_gather | solution.py:29
  8.6 121.2 %all-gather.12.cloned.1.call-start = ((), (), s32[]{:S(2)}) async-start(), calls=%async_computation.5 | async-start | bytes 2621440 | tf_op jit(solution)/shard_map/all_gather | solution.py:33
  9.4 157.2 %all-gather.8.cloned.1.call-start = ((), (), s32[]{:S(2)}) async-start(), calls=%async_computation.3 | async-start | bytes 2621440 | tf_op jit(solution)/shard_map/all_gather | solution.py:10
  10.0 204.6 %all-gather.6.cloned.1.call-start = ((), (), s32[]{:S(2)}) async-start(), calls=%async_computation.2 | async-start | bytes 4718592 | tf_op jit(solution)/shard_map/all_gather | solution.py:30
  10.5 302.1 %reduce-scatter.3.cloned.1.call-start = ((), (), s32[]{:S(2)}) async-start(), calls=%async_computation.7 | async-start | bytes 9437184 | tf_op jit(solution)/shard_map/reduce_scatter | solution.py:54
  134.0 84.7 %copy-start.1 = (bf16[8192,128]{1,0:T(8,128)(2,1)S(1)}, bf16[8192,128]{1,0:T(8,128)(2,1)}, u32[]{:S(2)}) copy-start(bf16[8192,128]{1,0:T(8,128)(2,1)} %all-gather.14.cloned.1.call-done) | copy-start | bytes 6291460
  218.7 1.6 copy-start.2
  224.8 211.0 %reduce-scatter.5.cloned.1.call-start = ((), (), s32[]{:S(2)}) async-start(), calls=%async_computation.8 | async-start | bytes 15728640 | tf_op jit(solution)/shard_map/reduce_scatter | solution.py:16
  224.8 3.5 copy-start
  228.3 2.2 copy-start.3
Sparse Core Ops, SparseCore 0:
  9.8 35.8 all-gather.13
  47.3 46.4 all-gather.9
  95.7 34.1 all-gather.11
  131.6 34.9 all-gather.7
  168.0 46.4 all-gather.5
  224.9 87.6 reduce-scatter.2
  315.7 119.9 reduce-scatter.4
where the time goes:
time: 450 us; the launch traced here: 448 us
  waiting for transfers between devices  396 us (88%)
  matrix products  22.8 us (5%)
  between operations  14.2 us (3%)
  local copies, waits for them, and re-layouts  7.72 us (2%)
  other arithmetic  7.1 us (2%)
    reduce_scatter x1, waiting for transfers between devices, own_rows(): lax.psum_scatter(portion(jnp.int32(0), count), axis, scatter_dimension=0,...  121 us
    reduce_scatter x1, waiting for transfers between devices, body(): lax.psum_scatter(partial_term, 'tp', scatter_dimension=1, tiled=True)  76.3 us
    all_gather x1, waiting for transfers between devices, body(): whole = lax.all_gather(tokens, 'tp', axis=1, tiled=True)  48.1 us
    all_gather x1, waiting for transfers between devices, body(): grads = lax.all_gather(out_grad, 'tp', axis=1, tiled=True)  48 us
    all_gather x1, waiting for transfers between devices, body(): lax.all_gather(gate_weight, 'fsdp', axis=0, tiled=True)  35.1 us
    all_gather x1, waiting for transfers between devices, over_all(): lax.all_gather(a, axis, axis=dim, tiled=True)  32.6 us
    all_gather x1, waiting for transfers between devices, body(): lax.all_gather(up_weight, 'fsdp', axis=0, tiled=True)  31.9 us
  transfers between devices with their start and end apart: 7, of which 7 were waited for; matrix products, arithmetic and copies ran while one was open for 4% of the time, Pallas kernels for 0%

commit v1 on v0

v1 whole, which is shorter than its diff:
```python
import functools
import math

import jax
import jax.numpy as jnp
from jax import lax
from jax.sharding import PartitionSpec as P
from jax.experimental import pallas as pl
from jax.experimental.pallas import tpu as pltpu

MESH = pl.DeviceIdType.MESH
F32 = jnp.float32
BF16 = jnp.bfloat16
VMEM_LIMIT = 60 * 1024 * 1024


def place(nf, nt):
    return lax.axis_index("fsdp"), lax.axis_index("tp")


def enter(nf, nt):
    f, t = place(nf, nt)
    barrier = pltpu.get_barrier_semaphore()
    for j in range(1, nf):
        pl.semaphore_signal(
            barrier, inc=1, device_id=(lax.rem(f + j, nf), t), device_id_type=MESH
        )
    for j in range(1, nt):
        pl.semaphore_signal(
            barrier, inc=1, device_id=(f, lax.rem(t + j, nt)), device_id_type=MESH
        )
    pl.semaphore_wait(barrier, nf + nt - 2)


def remote(src, dst, send, recv, device):
    return pltpu.make_async_remote_copy(
        src_ref=src,
        dst_ref=dst,
        send_sem=send,
        recv_sem=recv,
        device_id=device,
        device_id_type=MESH,
    )


def line_steps(stage, mats, nz, f, t, up_send, down_send, recv, arrived):
    z = t // 2

    def up(m, b):
        return remote(
            stage.at[m, b], stage.at[m, b], up_send.at[m, b], recv.at[m, b], (f, t + 2)
        )

    def down(m, b):
        return remote(
            stage.at[m, b], stage.at[m, b], down_send.at[m, b], recv.at[m, b], (f, t - 2)
        )

    for s in range(nz):
        for m in range(mats):
            for direction in (0, 1) if s else (0,):
                b = z - s if direction == 0 else z + s

                @pl.when((b >= 0) & (b < nz))
                def _(m=m, b=b, s=s, direction=direction):
                    if s:
                        up(m, b).wait_recv()
                    if s == 0 or direction == 0:

                        @pl.when(z < nz - 1)
                        def _():
                            up(m, b).start()

                    if s == 0 or direction == 1:

                        @pl.when(z > 0)
                        def _():
                            down(m, b).start()

                    arrived(m, b)

    def finish():
        for b in range(nz):
            for m in range(mats):

                @pl.when((z < nz - 1) & (b <= z))
                def _(m=m, b=b):
                    up(m, b).wait_send()

                @pl.when((z > 0) & (b >= z))
                def _(m=m, b=b):
                    down(m, b).wait_send()

    return finish


def spread_kernel(
    nf,
    nt,
    tokens,
    grads,
    weights,
    x_out,
    g_out,
    w_out,
    stage,
    local_sem,
    up_send,
    down_send,
    line_recv,
    plane_send,
    plane_recv,
    pair_send,
    pair_recv,
    w_send,
    w_recv,
):
    f, t = place(nf, nt)
    nz = nt // 2
    z, k = t // 2, lax.rem(t, 2)
    rows, width = tokens.shape
    outs = (x_out, g_out)
    loads = []
    for m, ref in enumerate((tokens, grads)):
        load = pltpu.make_async_copy(ref, stage.at[m, z], local_sem.at[m])
        load.start()
        loads.append(load)
    part = w_out.shape[0]
    depth = weights.shape[1]
    w_own = pltpu.make_async_copy(
        weights.at[pl.ds(t * part, part)],
        w_out.at[:, pl.ds(pl.multiple_of(t * depth, depth), depth)],
        local_sem.at[2],
    )
    w_own.start()
    enter(nf, nt)
    for load in loads:
        load.wait()

    half = pl.ds(pl.multiple_of(k * width, width), width)

    def spot(m, g):
        return outs[m].at[pl.ds(pl.multiple_of(g * rows, rows), rows), half]

    def plane(m, b):
        return remote(
            stage.at[m, b], spot(m, f), plane_send.at[m, b], plane_recv.at[m, f], (b, t)
        )

    def plane_in(m, g):
        return remote(
            stage.at[m, 0], spot(m, g), plane_send.at[m, 0], plane_recv.at[m, g], (f, t)
        )

    def keep(m):
        return pltpu.make_async_copy(stage.at[m, f], spot(m, f), plane_recv.at[m, f])

    def arrived(m, b):
        @pl.when(b != f)
        def _():
            plane(m, b).start()

        @pl.when(b == f)
        def _():
            keep(m).start()

    finish = line_steps(
        stage, 2, nz, f, t, up_send, down_send, line_recv, arrived
    )

    def w_copy(u):
        return remote(
            weights.at[pl.ds(u * part, part)],
            w_out.at[:, pl.ds(pl.multiple_of(t * depth, depth), depth)],
            w_send.at[u],
            w_recv.at[t],
            (f, u),
        )

    def w_in(u):
        return remote(
            weights.at[pl.ds(0, part)],
            w_out.at[:, pl.ds(pl.multiple_of(u * depth, depth), depth)],
            w_send.at[u],
            w_recv.at[u],
            (f, u),
        )

    for j in range(1, nt):
        w_copy(lax.rem(t + j, nt)).start()

    def pair(m, g):
        return remote(
            spot(m, g), spot(m, g), pair_send.at[m, g], pair_recv.at[m, g], (f, t + 1 - 2 * k)
        )

    for m in range(2):
        for j in range(nf):
            g = lax.rem(f + j, nf)
            if j == 0:
                keep(m).wait()
            else:
                plane_in(m, g).wait_recv()
            pair(m, g).start()
    finish()
    for m in range(2):
        for b in range(nz):

            @pl.when(b != f)
            def _(m=m, b=b):
                plane(m, b).wait_send()

        for g in range(nf):
            pair(m, g).wait()
    w_own.wait()
    for j in range(1, nt):
        u = lax.rem(t + j, nt)
        w_copy(u).wait_send()
        w_in(u).wait_recv()


def middle_kernel(
    nf,
    nt,
    partial,
    all_out,
    hidden_out,
    landing,
    stage,
    hidden_own,
    sum_send,
    sum_recv,
    up_send,
    down_send,
    line_recv,
    plane_send,
    plane_recv,
    pair_send,
    pair_recv,
    h_send,
    h_recv,
    local_sem,
):
    f, t = place(nf, nt)
    nz = nt // 2
    z, k = t // 2, lax.rem(t, 2)
    rows = landing.shape[1]
    width = hidden_own.shape[1]

    def block(g):
        return pl.ds(pl.multiple_of(g * rows, rows), rows)

    enter(nf, nt)

    def share(g):
        return remote(
            partial.at[block(g)], landing.at[f], sum_send.at[g], sum_recv.at[f], (g, t)
        )

    def share_in(g):
        return remote(
            partial.at[block(g)], landing.at[g], sum_send.at[g], sum_recv.at[g], (g, t)
        )

    for j in range(1, nf):
        share(lax.rem(f + j, nf)).start()
    for j in range(1, nf):
        share_in(lax.rem(f + j, nf)).wait_recv()
    total = partial[block(f), :]
    for j in range(1, nf):
        total = total + landing[lax.rem(f + j, nf)]
    gate = total[:, :width]
    up = total[:, width : 2 * width]
    hidden_grad = total[:, 2 * width :]
    squashed = jax.nn.sigmoid(gate)
    activated = gate * squashed
    slope = squashed * (1.0 + gate * (1.0 - squashed))
    stage[0, z, :, :width] = (hidden_grad * up * slope).astype(BF16)
    stage[0, z, :, width:] = (hidden_grad * activated).astype(BF16)
    hidden_own[...] = (activated * up).astype(BF16)

    def h_copy(g):
        return remote(
            hidden_own, hidden_out.at[block(f)], h_send.at[g], h_recv.at[f], (g, t)
        )

    def h_in(g):
        return remote(
            hidden_own, hidden_out.at[block(g)], h_send.at[g], h_recv.at[g], (g, t)
        )

    def spot(g, b):
        at = pl.multiple_of((2 * b + k) * 2 * width, 2 * width)
        return all_out.at[block(g), pl.ds(at, 2 * width)]

    def plane(b, g):
        return remote(
            stage.at[0, b], spot(f, b), plane_send.at[b, g], plane_recv.at[b, f], (g, t)
        )

    def plane_in(b, g):
        return remote(
            stage.at[0, b], spot(g, b), plane_send.at[b, g], plane_recv.at[b, g], (g, t)
        )

    def keep(b):
        return pltpu.make_async_copy(stage.at[0, b], spot(f, b), plane_recv.at[b, f])

    def arrived(m, b):
        for j in range(1, nf):
            plane(b, lax.rem(f + j, nf)).start()
        keep(b).start()

    finish = line_steps(stage, 1, nz, f, t, up_send, down_send, line_recv, arrived)
    for j in range(1, nf):
        h_copy(lax.rem(f + j, nf)).start()
    h_keep = pltpu.make_async_copy(hidden_own, hidden_out.at[block(f)], local_sem.at[0])
    h_keep.start()

    def pair(b, g):
        return remote(
            spot(g, b), spot(g, b), pair_send.at[b, g], pair_recv.at[b, g], (f, t + 1 - 2 * k)
        )

    def pair_in(b, g):
        at = pl.multiple_of((2 * b + 1 - k) * 2 * width, 2 * width)
        here = all_out.at[block(g), pl.ds(at, 2 * width)]
        return remote(
            here, here, pair_send.at[b, g], pair_recv.at[b, g], (f, t + 1 - 2 * k)
        )

    for b in range(nz):
        for j in range(nf):
            g = lax.rem(f + j, nf)
            if j == 0:
                keep(b).wait()
            else:
                plane_in(b, g).wait_recv()
            pair(b, g).start()
    finish()
    h_keep.wait()
    for j in range(1, nf):
        g = lax.rem(f + j, nf)
        share(g).wait_send()
        h_copy(g).wait_send()
        h_in(g).wait_recv()
        for b in range(nz):
            plane(b, g).wait_send()
    for b in range(nz):
        for g in range(nf):
            pair(b, g).wait_send()
            pair_in(b, g).wait_recv()


def return_kernel(nf, nt, result, out, landing, send, recv, send2, recv2, local_sem):
    f, t = place(nf, nt)
    rows = landing.shape[1]

    def block(g):
        return pl.ds(pl.multiple_of(g * rows, rows), rows)

    keep = pltpu.make_async_copy(result.at[block(f)], landing.at[f], local_sem.at[0])
    keep.start()
    enter(nf, nt)

    def first(g):
        return remote(result.at[block(g)], landing.at[f], send.at[g], recv.at[f], (g, t))

    def first_in(g):
        return remote(result.at[block(g)], landing.at[g], send.at[g], recv.at[g], (g, t))

    for j in range(1, nf):
        first(lax.rem(f + j, nf)).start()
    keep.wait()
    lane = lax.rem(t, nf)

    def second(g):
        return remote(
            landing.at[g], out.at[lane], send2.at[g], recv2.at[lane], (f, 2 * g + t // nf)
        )

    def own(g):
        return pltpu.make_async_copy(landing.at[g], out.at[lane], recv2.at[lane])

    def second_in(i):
        return remote(
            landing.at[0], out.at[i], send2.at[0], recv2.at[i], (f, t)
        )

    for j in range(nf):
        g = lax.rem(f + j, nf)
        if j:
            first_in(g).wait_recv()

        @pl.when(2 * g + t // nf != t)
        def _(g=g):
            second(g).start()

        @pl.when(2 * g + t // nf == t)
        def _(g=g):
            own(g).start()

    source = lax.rem(t, 2) * nf
    for i in range(nf):

        @pl.when(source + i != t)
        def _(i=i):
            second_in(i).wait_recv()

        @pl.when(source + i == t)
        def _(i=i):
            own(0).wait()

    for j in range(nf):
        g = lax.rem(f + j, nf)
        if j:
            first(g).wait_send()

        @pl.when(2 * g + t // nf != t)
        def _(g=g):
            second(g).wait_send()


def params(number):
    return pltpu.CompilerParams(
        collective_id=number, has_side_effects=True, vmem_limit_bytes=VMEM_LIMIT
    )


ANY = pl.BlockSpec(memory_space=pl.ANY)
VMEM = pl.BlockSpec(memory_space=pltpu.VMEM)
DMA = pltpu.SemaphoreType.DMA


def body(tokens, out_grad, gate_weight, up_weight, down_weight):
    nf, nt = lax.axis_size("fsdp"), lax.axis_size("tp")
    nz = nt // 2
    rows, shard = tokens.shape
    depth, width = gate_weight.shape
    count = rows * nf
    factor = 1.0 / math.sqrt(count)
    assert nt == 2 * nf and depth == 2 * shard

    pairs = jnp.concatenate([gate_weight, up_weight], axis=1)
    part = depth // nt
    whole, grads, turned = pl.pallas_call(
        functools.partial(spread_kernel, nf, nt),
        out_shape=(
            jax.ShapeDtypeStruct((count, depth), BF16),
            jax.ShapeDtypeStruct((count, depth), BF16),
            jax.ShapeDtypeStruct((part, nt * 2 * width), BF16),
        ),
        in_specs=[VMEM, VMEM, VMEM],
        out_specs=(VMEM, VMEM, VMEM),
        scratch_shapes=[
            pltpu.VMEM((2, nz, rows, shard), BF16),
            DMA((3,)),
            DMA((2, nz)),
            DMA((2, nz)),
            DMA((2, nz)),
            DMA((2, nz)),
            DMA((2, nf)),
            DMA((2, nf)),
            DMA((2, nf)),
            DMA((nt,)),
            DMA((nt,)),
        ],
        compiler_params=params(0),
        name="spread",
    )(tokens, out_grad, pairs)

    both = jnp.dot(whole, pairs, preferred_element_type=F32)
    back = lax.dot_general(
        grads, down_weight, (((1,), (1,)), ((), ())), preferred_element_type=F32
    )
    partial = jnp.concatenate([both, back], axis=1)

    deltas, hidden = pl.pallas_call(
        functools.partial(middle_kernel, nf, nt),
        out_shape=(
            jax.ShapeDtypeStruct((count, nt * 2 * width), BF16),
            jax.ShapeDtypeStruct((count, width), BF16),
        ),
        in_specs=[VMEM],
        out_specs=(VMEM, VMEM),
        scratch_shapes=[
            pltpu.VMEM((nf, rows, 3 * width), F32),
            pltpu.VMEM((1, nz, rows, 2 * width), BF16),
            pltpu.VMEM((rows, width), BF16),
            DMA((nf,)),
            DMA((nf,)),
            DMA((1, nz)),
            DMA((1, nz)),
            DMA((1, nz)),
            DMA((nz, nf)),
            DMA((nz, nf)),
            DMA((nz, nf)),
            DMA((nz, nf)),
            DMA((nf,)),
            DMA((nf,)),
            DMA((1,)),
        ],
        compiler_params=params(1),
        name="middle",
    )(partial)

    piece = lax.dot_general(
        deltas, turned, (((1,), (1,)), ((), ())), preferred_element_type=F32
    ).astype(BF16)
    input_grad = pl.pallas_call(
        functools.partial(return_kernel, nf, nt),
        out_shape=jax.ShapeDtypeStruct((nf, rows, part), BF16),
        in_specs=[VMEM],
        out_specs=VMEM,
        scratch_shapes=[
            pltpu.VMEM((nf, rows, part), BF16),
            DMA((nf,)),
            DMA((nf,)),
            DMA((nf,)),
            DMA((nf,)),
            DMA((1,)),
        ],
        compiler_params=params(2),
        name="back",
    )(piece)
    input_grad = input_grad.transpose(1, 0, 2).reshape(rows, shard)

    own = lax.dynamic_slice_in_dim(deltas, lax.axis_index("tp") * 2 * width, 2 * width, 1)
    contract = (((0,), (0,)), ((), ()))
    gate_grad = factor * lax.dot_general(
        whole, own[:, :width], contract, preferred_element_type=F32
    )
    up_grad = factor * lax.dot_general(
        whole, own[:, width:], contract, preferred_element_type=F32
    )
    down_grad = factor * lax.dot_general(hidden, grads, contract, preferred_element_type=F32)
    return (input_grad, gate_grad, up_grad, down_grad)


def solution(mesh):
    return jax.shard_map(
        body,
        mesh=mesh,
        in_specs=(
            P("fsdp", "tp"),
            P("fsdp", "tp"),
            P("fsdp", "tp"),
            P("fsdp", "tp"),
            P("tp", "fsdp"),
        ),
        out_specs=(P("fsdp", "tp"), P("fsdp", "tp"), P("fsdp", "tp"), P("tp", "fsdp")),
        check_vma=False,
    )
```

time: 450 us -> 227 us (0.50)
  waiting for transfers between devices: 396 us -> 0 us
  Pallas kernels: 0 us -> 198 us
  between operations: 14.2 us -> 0.75 us
  other arithmetic: 7.1 us -> 1.28 us
    pallas_call x0 -> x3, Pallas kernels: none -> 198 us  [the longest x1 98.1 us: body(): pl.pallas_call(functools.partial(spread_kernel, nf, nt), out_shape=(jax.S...]
    reduce_scatter x2 -> x0, waiting for transfers between devices: 197 us -> none  [the longest x1 121 us: own_rows(): lax.psum_scatter(portion(jnp.int32(0), count), axis, scatter_dimension=0,...]
    all_gather x5 -> x0, waiting for transfers between devices: 196 us -> none  [the longest x1 48.1 us: body(): whole = lax.all_gather(tokens, 'tp', axis=1, tiled=True)]
    dot_general x8 -> x6, matrix products: 22.8 us -> 19.9 us  [the longest x1 4.62 us: body(): lax.dot_general(whole, own[:, width:], contract, preferred_element_type=F32)]
  transfers between devices with their start and end apart: 7 -> 0, of which waited for: 7 -> 0; matrix products, arithmetic and copies ran while one was open for 4% -> 0% of each run, Pallas kernels for 0% -> 0%
where the time goes in v1:
time: 227 us; the launch traced here: 226 us
  Pallas kernels  198 us (87%)
  matrix products  19.9 us (9%)
  local copies, waits for them, and re-layouts  5.7 us (3%)
    pallas_call x1, Pallas kernels, body(): pl.pallas_call(functools.partial(spread_kernel, nf, nt), out_shape=(jax.S...  98.1 us
    pallas_call x1, Pallas kernels, body(): pl.pallas_call(functools.partial(middle_kernel, nf, nt), out_shape=(jax.S...  74.7 us
    pallas_call x1, Pallas kernels, body(): pl.pallas_call(functools.partial(return_kernel, nf, nt), out_shape=jax.Sh...  25.5 us
    dot_general x1, matrix products, body(): lax.dot_general(whole, own[:, width:], contract, preferred_element_type=F32)  4.62 us

profile of v1, /device:TPU:13, one launch (start us, length us, event | category | flops | bytes accessed | tf_op | source)
XLA Modules:
  0.0 225.9 jit_solution(11230065216624195736)
XLA Ops:
  0.6 0.0 copy-start
  0.6 1.2 constant_dynamic-update-slice_fusion.1
  1.8 1.2 constant_dynamic-update-slice_fusion.weights
  3.0 0.0 copy-start.3
  3.0 1.0 copy-done.3
  4.0 98.1 %spread.1 = (bf16[1024,2048]{1,0:T(8,128)(2,1)}, bf16[1024,2048]{1,0:T(8,128)(2,1)}, bf16[256,2048]{1,0:T(8,128)(2,1)}) custom-call(bf16[256,1024]{1,0:T(8,128)(2,1)} %tokens.1, bf16[256,1024]{1,0:T(8,128)(2,1)} %grads.1, bf16[2048,256]{1,0:T(8,128)(2,1)} %copy-done.3), custom_call_target="tpu_custom_call" | custom-call | tf_op jit(solution)/shard_map/spread/pallas_call | solution.py:446
  102.1 0.0 copy-start.2
  102.1 0.0 copy-start.4
  102.1 0.0 copy-done
  102.1 3.6 %fusion.5 = f32[1024,128]{1,0:T(8,128)S(1)} fusion(bf16[1024,2048]{1,0:T(8,128)(2,1)} %get-tuple-element.10, bf16[128,2048]{1,0:T(8,128)(2,1)S(1)} %copy-done), kind=kOutput, calls=%fused_computation.12 | convolution fusion | flops 536870912 | bytes 5242880 | tf_op jit(solution)/shard_map/dot_general | solution.py:473
  105.7 0.0 copy-done.2
  105.8 0.1 copy-done.4
  105.9 1.3 fusion.4
  107.1 0.0 copy-start.6
  107.1 1.3 pad_maximum_fusion.partial
  108.4 74.7 %middle.1 = (bf16[1024,2048]{1,0:T(8,128)(2,1)}, bf16[1024,128]{1,0:T(8,128)(2,1)}) custom-call(f32[1024,384]{1,0:T(8,128)} %pad_maximum_fusion.partial), custom_call_target="tpu_custom_call" | custom-call | tf_op jit(solution)/shard_map/middle/pallas_call | solution.py:478
  183.1 0.0 copy-done.6
  183.1 4.3 %convolution_convert_fusion.result = bf16[1024,256]{1,0:T(8,128)(2,1)} fusion(bf16[1024,2048]{1,0:T(8,128)(2,1)} %get-tuple-element.11, bf16[256,2048]{1,0:T(8,128)(2,1)S(1)} %copy-done.6), kind=kOutput, calls=%fused_computation.4 | convolution fusion | flops 1074003968 | bytes 5767168 | tf_op jit(solution)/shard_map/dot_general | solution.py:507
  187.4 25.5 %back.1 = bf16[4,256,256]{2,1,0:T(8,128)(2,1)} custom-call(bf16[1024,256]{1,0:T(8,128)(2,1)} %convolution_convert_fusion.result), custom_call_target="tpu_custom_call" | custom-call | tf_op jit(solution)/shard_map/back/pallas_call | solution.py:510
  212.9 1.2 copy.13
  214.1 1.0 copy.14
  215.1 4.5 %convolution_multiply_fusion.2 = f32[2048,128]{1,0:T(8,128)} fusion(bf16[1024,2048]{1,0:T(8,128)(2,1)} %get-tuple-element.9, bf16[1024,2048]{1,0:T(8,128)(2,1)} %get-tuple-element.11, s32[]{:T(128)S(6)} %select_n.3), kind=kOutput, calls=%fused_computation.2 | convolution fusion | flops 537133056 | bytes 5505028 | tf_op jit(solution)/shard_map/dot_general | solution.py:530
  219.6 0.0 copy-start.5
  219.6 0.0 copy-start.1
  219.6 4.6 %convolution_multiply_fusion.1 = f32[2048,128]{1,0:T(8,128)} fusion(bf16[1024,2048]{1,0:T(8,128)(2,1)} %get-tuple-element.9, bf16[1024,2048]{1,0:T(8,128)(2,1)} %get-tuple-element.11, s32[]{:T(128)S(6)} %add.4), kind=kOutput, calls=%fused_computation.1 | convolution fusion | flops 537133056 | bytes 5505028 | tf_op jit(solution)/shard_map/dot_general | solution.py:533
  224.2 0.0 copy-done.5
  224.2 0.0 copy-done.1
  224.2 1.7 convolution_multiply_fusion
Async XLA Ops:
  0.6 101.5 %copy-start = (bf16[128,2048]{1,0:T(8,128)(2,1)S(1)}, bf16[128,2048]{1,0:T(8,128)(2,1)}, u32[]{:S(2)}) copy-start(bf16[128,2048]{1,0:T(8,128)(2,1)} %param.9) | copy-start | bytes 1572868
  3.0 1.0 copy-start.3
  102.1 3.6 %copy-start.2 = (bf16[1024,2048]{1,0:T(8,128)(2,1)S(1)}, bf16[1024,2048]{1,0:T(8,128)(2,1)}, u32[]{:S(2)}) copy-start(bf16[1024,2048]{1,0:T(8,128)(2,1)} %get-tuple-element.9) | copy-start | bytes 12582916
  102.1 3.7 %copy-start.4 = (bf16[2048,256]{1,0:T(8,128)(2,1)S(1)}, bf16[2048,256]{1,0:T(8,128)(2,1)}, u32[]{:S(2)}) copy-start(bf16[2048,256]{1,0:T(8,128)(2,1)} %copy-done.3) | copy-start | bytes 3145732
  107.1 76.0 %copy-start.6 = (bf16[256,2048]{1,0:T(8,128)(2,1)S(1)}, bf16[256,2048]{1,0:T(8,128)(2,1)}, u32[]{:S(2)}) copy-start(bf16[256,2048]{1,0:T(8,128)(2,1)} %get-tuple-element.12) | copy-start | bytes 3145732
  219.6 4.6 %copy-start.5 = (bf16[1024,128]{1,0:T(8,128)(2,1)S(1)}, bf16[1024,128]{1,0:T(8,128)(2,1)}, u32[]{:S(2)}) copy-start(bf16[1024,128]{1,0:T(8,128)(2,1)} %get-tuple-element.13) | copy-start | bytes 786436
  219.6 4.6 %copy-start.1 = (bf16[1024,2048]{1,0:T(8,128)(2,1)S(1)}, bf16[1024,2048]{1,0:T(8,128)(2,1)}, u32[]{:S(2)}) copy-start(bf16[1024,2048]{1,0:T(8,128)(2,1)} %get-tuple-element.10) | copy-start | bytes 12582916

commit v2 on v1

--- a/solution.py
+++ b/solution.py
@@ -99,10 +99,8 @@
     nt,
     tokens,
     grads,
-    weights,
     x_out,
     g_out,
-    w_out,
     stage,
     local_sem,
     up_send,
@@ -112,8 +110,6 @@
     plane_recv,
     pair_send,
     pair_recv,
-    w_send,
-    w_recv,
 ):
     f, t = place(nf, nt)
     nz = nt // 2
@@ -125,14 +121,6 @@
         load = pltpu.make_async_copy(ref, stage.at[m, z], local_sem.at[m])
         load.start()
         loads.append(load)
-    part = w_out.shape[0]
-    depth = weights.shape[1]
-    w_own = pltpu.make_async_copy(
-        weights.at[pl.ds(t * part, part)],
-        w_out.at[:, pl.ds(pl.multiple_of(t * depth, depth), depth)],
-        local_sem.at[2],
-    )
-    w_own.start()
     enter(nf, nt)
     for load in loads:
         load.wait()
@@ -167,27 +155,6 @@
     finish = line_steps(
         stage, 2, nz, f, t, up_send, down_send, line_recv, arrived
     )
-
-    def w_copy(u):
-        return remote(
-            weights.at[pl.ds(u * part, part)],
-            w_out.at[:, pl.ds(pl.multiple_of(t * depth, depth), depth)],
-            w_send.at[u],
-            w_recv.at[t],
-            (f, u),
-        )
-
-    def w_in(u):
-        return remote(
-            weights.at[pl.ds(0, part)],
-            w_out.at[:, pl.ds(pl.multiple_of(u * depth, depth), depth)],
-            w_send.at[u],
-            w_recv.at[u],
-            (f, u),
-        )
-
-    for j in range(1, nt):
-        w_copy(lax.rem(t + j, nt)).start()
 
     def pair(m, g):
         return remote(
@@ -212,19 +179,16 @@
 
         for g in range(nf):
             pair(m, g).wait()
-    w_own.wait()
-    for j in range(1, nt):
-        u = lax.rem(t + j, nt)
-        w_copy(u).wait_send()
-        w_in(u).wait_recv()
 
 
 def middle_kernel(
     nf,
     nt,
     partial,
+    weights,
     all_out,
     hidden_out,
+    w_out,
     landing,
     stage,
     hidden_own,
@@ -240,6 +204,8 @@
     h_send,
     h_recv,
     local_sem,
+    w_send,
+    w_recv,
 ):
     f, t = place(nf, nt)
     nz = nt // 2
@@ -250,6 +216,14 @@
     def block(g):
         return pl.ds(pl.multiple_of(g * rows, rows), rows)
 
+    part = w_out.shape[0]
+    depth = weights.shape[1]
+    w_own = pltpu.make_async_copy(
+        weights.at[pl.ds(t * part, part)],
+        w_out.at[:, pl.ds(pl.multiple_of(t * depth, depth), depth)],
+        local_sem.at[1],
+    )
+    w_own.start()
     enter(nf, nt)
 
     def share(g):
@@ -264,6 +238,28 @@
 
     for j in range(1, nf):
         share(lax.rem(f + j, nf)).start()
+
+    def w_copy(u):
+        return remote(
+            weights.at[pl.ds(u * part, part)],
+            w_out.at[:, pl.ds(pl.multiple_of(t * depth, depth), depth)],
+            w_send.at[u],
+            w_recv.at[t],
+            (f, u),
+        )
+
+    def w_in(u):
+        return remote(
+            weights.at[pl.ds(0, part)],
+            w_out.at[:, pl.ds(pl.multiple_of(u * depth, depth), depth)],
+            w_send.at[u],
+            w_recv.at[u],
+            (f, u),
+        )
+
+    for j in range(1, nt):
+        w_copy(lax.rem(t + j, nt)).start()
+
     for j in range(1, nf):
         share_in(lax.rem(f + j, nf)).wait_recv()
     total = partial[block(f), :]
@@ -350,6 +346,11 @@
         for g in range(nf):
             pair(b, g).wait_send()
             pair_in(b, g).wait_recv()
+    w_own.wait()
+    for j in range(1, nt):
+        u = lax.rem(t + j, nt)
+        w_copy(u).wait_send()
+        w_in(u).wait_recv()
 
 
 def return_kernel(nf, nt, result, out, landing, send, recv, send2, recv2, local_sem):
@@ -443,18 +444,17 @@
 
     pairs = jnp.concatenate([gate_weight, up_weight], axis=1)
     part = depth // nt
-    whole, grads, turned = pl.pallas_call(
+    whole, grads = pl.pallas_call(
         functools.partial(spread_kernel, nf, nt),
         out_shape=(
             jax.ShapeDtypeStruct((count, depth), BF16),
             jax.ShapeDtypeStruct((count, depth), BF16),
-            jax.ShapeDtypeStruct((part, nt * 2 * width), BF16),
         ),
-        in_specs=[VMEM, VMEM, VMEM],
-        out_specs=(VMEM, VMEM, VMEM),
+        in_specs=[VMEM, VMEM],
+        out_specs=(VMEM, VMEM),
         scratch_shapes=[
             pltpu.VMEM((2, nz, rows, shard), BF16),
-            DMA((3,)),
+            DMA((2,)),
             DMA((2, nz)),
             DMA((2, nz)),
             DMA((2, nz)),
@@ -462,12 +462,10 @@
             DMA((2, nf)),
             DMA((2, nf)),
             DMA((2, nf)),
-            DMA((nt,)),
-            DMA((nt,)),
         ],
         compiler_params=params(0),
         name="spread",
-    )(tokens, out_grad, pairs)
+    )(tokens, out_grad)
 
     both = jnp.dot(whole, pairs, preferred_element_type=F32)
     back = lax.dot_general(
@@ -475,14 +473,15 @@
     )
     partial = jnp.concatenate([both, back], axis=1)
 
-    deltas, hidden = pl.pallas_call(
+    deltas, hidden, turned = pl.pallas_call(
         functools.partial(middle_kernel, nf, nt),
         out_shape=(
             jax.ShapeDtypeStruct((count, nt * 2 * width), BF16),
             jax.ShapeDtypeStruct((count, width), BF16),
+            jax.ShapeDtypeStruct((part, nt * 2 * width), BF16),
         ),
-        in_specs=[VMEM],
-        out_specs=(VMEM, VMEM),
+        in_specs=[VMEM, VMEM],
+        out_specs=(VMEM, VMEM, VMEM),
         scratch_shapes=[
             pltpu.VMEM((nf, rows, 3 * width), F32),
             pltpu.VMEM((1, nz, rows, 2 * width), BF16),
@@ -498,11 +497,13 @@
             DMA((nz, nf)),
             DMA((nf,)),
             DMA((nf,)),
-            DMA((1,)),
+            DMA((2,)),
+            DMA((nt,)),
+            DMA((nt,)),
         ],
         compiler_params=params(1),
         name="middle",
-    )(partial)
+    )(partial, pairs)
 
     piece = lax.dot_general(
         deltas, turned, (((1,), (1,)), ((), ())), preferred_element_type=F32

time: 227 us -> 222 us (0.978)
    pallas_call x1, Pallas kernels: 98.1 us -> 75.4 us  [body(): pl.pallas_call(functools.partial(spread_kernel, nf, nt), out_shape=(jax.S...]
    pallas_call x1, Pallas kernels: 74.7 us -> 91.8 us  [body(): pl.pallas_call(functools.partial(middle_kernel, nf, nt), out_shape=(jax.S...]
    pallas_call x1, Pallas kernels: 25.5 us -> 28.9 us  [body(): pl.pallas_call(functools.partial(return_kernel, nf, nt), out_shape=jax.Sh...]
    dot_general x1, matrix products: 1.25 us -> 3.9 us  [body(): both = jnp.dot(whole, pairs, preferred_element_type=F32)]
    dot_general x1, matrix products: 3.6 us -> 1.25 us  [body(): lax.dot_general(grads, down_weight, (((1,), (1,)), ((), ())), preferred_e...]
where the time goes in v2:
time: 222 us
  Pallas kernels  196 us (88%)
  matrix products  19.2 us (9%)
  local copies, waits for them, and re-layouts  4.74 us (2%)
    pallas_call x1, Pallas kernels, body(): pl.pallas_call(functools.partial(middle_kernel, nf, nt), out_shape=(jax.S...  91.8 us
    pallas_call x1, Pallas kernels, body(): pl.pallas_call(functools.partial(spread_kernel, nf, nt), out_shape=(jax.S...  75.4 us
    pallas_call x1, Pallas kernels, body(): pl.pallas_call(functools.partial(return_kernel, nf, nt), out_shape=jax.Sh...  28.9 us
    dot_general x1, matrix products, body(): lax.dot_general(whole, own[:, width:], contract, preferred_element_type=F32)  4.62 us

profile of v2, /device:TPU:13, one launch (start us, length us, event | category | flops | bytes accessed | tf_op | source)
XLA Modules:
  0.0 222.0 jit_solution(13207436367849435883)
XLA Ops:
  0.6 0.0 copy-start
  0.6 75.4 %spread.1 = (bf16[1024,2048]{1,0:T(8,128)(2,1)}, bf16[1024,2048]{1,0:T(8,128)(2,1)}) custom-call(bf16[256,1024]{1,0:T(8,128)(2,1)} %tokens.1, bf16[256,1024]{1,0:T(8,128)(2,1)} %grads.1), custom_call_target="tpu_custom_call" | custom-call | tf_op jit(solution)/shard_map/spread/pallas_call | solution.py:447
  76.0 1.1 constant_dynamic-update-slice_fusion.1
  77.2 0.0 copy-start.1
  77.2 1.3 constant_dynamic-update-slice_fusion.weights
  78.5 0.0 copy-start.3
  78.5 3.9 %fusion.4 = f32[1024,256]{1,0:T(8,128)S(1)} fusion(bf16[1024,2048]{1,0:T(8,128)(2,1)} %get-tuple-element.9, bf16[2048,256]{1,0:T(8,128)(2,1)S(1)} %constant_dynamic-update-slice_fusion.weights), kind=kOutput, calls=%fused_computation.11 | convolution fusion | flops 1073741824 | bytes 6291456 | tf_op jit(solution)/shard_map/dot_general | solution.py:470
  82.4 0.0 copy-done
  82.4 0.0 copy-done.1
  82.4 1.3 fusion.5
  83.7 0.0 copy-done.3
  83.7 1.3 pad_maximum_fusion.partial
  85.0 91.8 %middle.1 = (bf16[1024,2048]{1,0:T(8,128)(2,1)}, bf16[1024,128]{1,0:T(8,128)(2,1)}, bf16[256,2048]{1,0:T(8,128)(2,1)}) custom-call(f32[1024,384]{1,0:T(8,128)} %pad_maximum_fusion.partial, bf16[2048,256]{1,0:T(8,128)(2,1)} %copy-done.3), custom_call_target="tpu_custom_call" | custom-call | tf_op jit(solution)/shard_map/middle/pallas_call | solution.py:476
  176.8 0.0 copy-start.2
  176.8 4.6 %convolution_multiply_fusion.1 = f32[2048,128]{1,0:T(8,128)} fusion(bf16[1024,2048]{1,0:T(8,128)(2,1)} %get-tuple-element.9, bf16[1024,2048]{1,0:T(8,128)(2,1)} %get-tuple-element.11, s32[]{:T(128)S(6)} %add.4), kind=kOutput, calls=%fused_computation.1 | convolution fusion | flops 537133056 | bytes 5505028 | tf_op jit(solution)/shard_map/dot_general | solution.py:534
  181.5 0.0 copy-done.2
  181.5 0.0 copy-start.5
  181.5 0.0 copy-start.6
  181.5 3.4 %convolution_multiply_fusion.2 = f32[2048,128]{1,0:T(8,128)} fusion(bf16[1024,2048]{1,0:T(8,128)(2,1)S(1)} %copy-done.2, bf16[1024,2048]{1,0:T(8,128)(2,1)} %get-tuple-element.11, s32[]{:T(128)S(6)} %select_n.3), kind=kOutput, calls=%fused_computation.2 | convolution fusion | flops 537133056 | bytes 5505028 | tf_op jit(solution)/shard_map/dot_general | solution.py:531
  184.9 0.0 copy-done.5
  184.9 0.0 copy-done.6
  184.9 0.0 copy-start.4
  184.9 2.1 convolution_convert_fusion.result
  187.0 28.9 %back.1 = bf16[4,256,256]{2,1,0:T(8,128)(2,1)} custom-call(bf16[1024,256]{1,0:T(8,128)(2,1)} %convolution_convert_fusion.result), custom_call_target="tpu_custom_call" | custom-call | tf_op jit(solution)/shard_map/back/pallas_call | solution.py:511
  215.9 1.2 copy.13
  217.1 1.0 copy.14
  218.1 0.0 copy-done.4
  218.1 3.9 %convolution_multiply_fusion = f32[128,2048]{1,0:T(8,128)} fusion(bf16[1024,128]{1,0:T(8,128)(2,1)S(1)} %copy-done.4, bf16[1024,2048]{1,0:T(8,128)(2,1)} %get-tuple-element.10), kind=kOutput, calls=%fused_computation | convolution fusion | flops 537133056 | bytes 5505024 | tf_op jit(solution)/shard_map/dot_general | solution.py:537
Async XLA Ops:
  0.6 81.8 %copy-start = (bf16[128,2048]{1,0:T(8,128)(2,1)S(1)}, bf16[128,2048]{1,0:T(8,128)(2,1)}, u32[]{:S(2)}) copy-start(bf16[128,2048]{1,0:T(8,128)(2,1)} %param.9) | copy-start | bytes 1572868
  77.2 5.3 %copy-start.1 = (bf16[1024,2048]{1,0:T(8,128)(2,1)S(1)}, bf16[1024,2048]{1,0:T(8,128)(2,1)}, u32[]{:S(2)}) copy-start(bf16[1024,2048]{1,0:T(8,128)(2,1)} %get-tuple-element.10) | copy-start | bytes 12582916
  78.5 5.2 %copy-start.3 = (bf16[2048,256]{1,0:T(8,128)(2,1)}, bf16[2048,256]{1,0:T(8,128)(2,1)S(1)}, u32[]{:S(2)}) copy-start(bf16[2048,256]{1,0:T(8,128)(2,1)S(1)} %constant_dynamic-update-slice_fusion.weights) | copy-start | bytes 3145732
  176.8 4.6 %copy-start.2 = (bf16[1024,2048]{1,0:T(8,128)(2,1)S(1)}, bf16[1024,2048]{1,0:T(8,128)(2,1)}, u32[]{:S(2)}) copy-start(bf16[1024,2048]{1,0:T(8,128)(2,1)} %get-tuple-element.9) | copy-start | bytes 12582916
  181.5 3.4 %copy-start.5 = (bf16[1024,2048]{1,0:T(8,128)(2,1)S(1)}, bf16[1024,2048]{1,0:T(8,128)(2,1)}, u32[]{:S(2)}) copy-start(bf16[1024,2048]{1,0:T(8,128)(2,1)} %get-tuple-element.11) | copy-start | bytes 12582916
  181.5 3.4 %copy-start.6 = (bf16[256,2048]{1,0:T(8,128)(2,1)S(1)}, bf16[256,2048]{1,0:T(8,128)(2,1)}, u32[]{:S(2)}) copy-start(bf16[256,2048]{1,0:T(8,128)(2,1)} %get-tuple-element.12) | copy-start | bytes 3145732
  184.9 33.3 %copy-start.4 = (bf16[1024,128]{1,0:T(8,128)(2,1)S(1)}, bf16[1024,128]{1,0:T(8,128)(2,1)}, u32[]{:S(2)}) copy-start(bf16[1024,128]{1,0:T(8,128)(2,1)} %get-tuple-element.13) | copy-start | bytes 786436

commit v3 on v2

--- a/solution.py
+++ b/solution.py
@@ -12,6 +12,8 @@
 F32 = jnp.float32
 BF16 = jnp.bfloat16
 VMEM_LIMIT = 60 * 1024 * 1024
+CHUNKS = 4
+AHEAD = 2
 
 
 def place(nf, nt):
@@ -115,6 +117,7 @@
     nz = nt // 2
     z, k = t // 2, lax.rem(t, 2)
     rows, width = tokens.shape
+    size = rows // CHUNKS
     outs = (x_out, g_out)
     loads = []
     for m, ref in enumerate((tokens, grads)):
@@ -127,58 +130,132 @@
 
     half = pl.ds(pl.multiple_of(k * width, width), width)
 
-    def spot(m, g):
-        return outs[m].at[pl.ds(pl.multiple_of(g * rows, rows), rows), half]
-
-    def plane(m, b):
-        return remote(
-            stage.at[m, b], spot(m, f), plane_send.at[m, b], plane_recv.at[m, f], (b, t)
-        )
-
-    def plane_in(m, g):
-        return remote(
-            stage.at[m, 0], spot(m, g), plane_send.at[m, 0], plane_recv.at[m, g], (f, t)
-        )
-
-    def keep(m):
-        return pltpu.make_async_copy(stage.at[m, f], spot(m, f), plane_recv.at[m, f])
-
-    def arrived(m, b):
+    def held(m, b, c):
+        return stage.at[m, b, pl.ds(c * size, size)]
+
+    def spot(m, g, c):
+        return outs[m].at[pl.ds(pl.multiple_of(g * rows + c * size, size), size), half]
+
+    def up(m, b, c):
+        here = held(m, b, c)
+        return remote(here, here, up_send.at[m, b, c], line_recv.at[m, b, c], (f, t + 2))
+
+    def down(m, b, c):
+        here = held(m, b, c)
+        return remote(here, here, down_send.at[m, b, c], line_recv.at[m, b, c], (f, t - 2))
+
+    def plane(m, b, c):
+        return remote(
+            held(m, b, c), spot(m, f, c), plane_send.at[m, b, c], plane_recv.at[m, f, c], (b, t)
+        )
+
+    def plane_in(m, g, c):
+        return remote(
+            held(m, 0, c), spot(m, g, c), plane_send.at[m, 0, c], plane_recv.at[m, g, c], (f, t)
+        )
+
+    def keep(m, c):
+        return pltpu.make_async_copy(held(m, f, c), spot(m, f, c), plane_recv.at[m, f, c])
+
+    def arrived(m, b, c):
         @pl.when(b != f)
         def _():
-            plane(m, b).start()
+            plane(m, b, c).start()
 
         @pl.when(b == f)
         def _():
-            keep(m).start()
-
-    finish = line_steps(
-        stage, 2, nz, f, t, up_send, down_send, line_recv, arrived
-    )
-
-    def pair(m, g):
-        return remote(
-            spot(m, g), spot(m, g), pair_send.at[m, g], pair_recv.at[m, g], (f, t + 1 - 2 * k)
-        )
-
-    for m in range(2):
-        for j in range(nf):
-            g = lax.rem(f + j, nf)
-            if j == 0:
-                keep(m).wait()
-            else:
-                plane_in(m, g).wait_recv()
-            pair(m, g).start()
-    finish()
-    for m in range(2):
-        for b in range(nz):
-
-            @pl.when(b != f)
-            def _(m=m, b=b):
-                plane(m, b).wait_send()
-
-        for g in range(nf):
-            pair(m, g).wait()
+            keep(m, c).start()
+
+    def send_own(c):
+        for m in range(2):
+
+            @pl.when(z < nz - 1)
+            def _(m=m):
+                up(m, z, c).start()
+
+            @pl.when(z > 0)
+            def _(m=m):
+                down(m, z, c).start()
+
+    def pair(m, g, c):
+        here = spot(m, g, c)
+        return remote(
+            here, here, pair_send.at[m, g, c], pair_recv.at[m, g, c], (f, t + 1 - 2 * k)
+        )
+
+    def swap(c):
+        for m in range(2):
+            for j in range(nf):
+                g = lax.rem(f + j, nf)
+                if j == 0:
+                    keep(m, c).wait()
+                else:
+                    plane_in(m, g, c).wait_recv()
+                pair(m, g, c).start()
+
+    edge = (z == 0) | (z == nz - 1)
+    for c in range(CHUNKS):
+        if c < AHEAD:
+            send_own(c)
+        else:
+
+            @pl.when(edge)
+            def _(c=c):
+                send_own(c)
+
+    for c in range(CHUNKS):
+        for m in range(2):
+            arrived(m, z, c)
+        for s in range(1, nz):
+            for direction in (0, 1):
+                b = z - s if direction == 0 else z + s
+
+                @pl.when((b >= 0) & (b < nz))
+                def _(b=b, direction=direction):
+                    for m in range(2):
+                        up(m, b, c).wait_recv()
+                        if direction == 0:
+
+                            @pl.when(z < nz - 1)
+                            def _():
+                                up(m, b, c).start()
+
+                        else:
+
+                            @pl.when(z > 0)
+                            def _():
+                                down(m, b, c).start()
+
+                        arrived(m, b, c)
+
+        if c + AHEAD < CHUNKS:
+
+            @pl.when(jnp.logical_not(edge))
+            def _(c=c):
+                send_own(c + AHEAD)
+
+        if c >= 2:
+            swap(c - 2)
+    for c in range(max(CHUNKS - 2, 0), CHUNKS):
+        swap(c)
+    for c in range(CHUNKS):
+        for m in range(2):
+            for b in range(nz):
+
+                @pl.when((z < nz - 1) & (b <= z))
+                def _(m=m, b=b):
+                    up(m, b, c).wait_send()
+
+                @pl.when((z > 0) & (b >= z))
+                def _(m=m, b=b):
+                    down(m, b, c).wait_send()
+
+                @pl.when(b != f)
+                def _(m=m, b=b):
+                    plane(m, b, c).wait_send()
+
+            for g in range(nf):
+                pair(m, g, c).wait()
 
 
 def middle_kernel(
@@ -455,13 +532,13 @@
         scratch_shapes=[
             pltpu.VMEM((2, nz, rows, shard), BF16),
             DMA((2,)),
-            DMA((2, nz)),
-            DMA((2, nz)),
-            DMA((2, nz)),
-            DMA((2, nz)),
-            DMA((2, nf)),
-            DMA((2, nf)),
-            DMA((2, nf)),
+            DMA((2, nz, CHUNKS)),
+            DMA((2, nz, CHUNKS)),
+            DMA((2, nz, CHUNKS)),
+            DMA((2, nz, CHUNKS)),
+            DMA((2, nf, CHUNKS)),
+            DMA((2, nf, CHUNKS)),
+            DMA((2, nf, CHUNKS)),
         ],
         compiler_params=params(0),
         name="spread",

time: 222 us -> 198 us (0.89)
  Pallas kernels: 196 us -> 171 us
    pallas_call x1, Pallas kernels: 91.8 us -> 65.6 us  [body(): pl.pallas_call(functools.partial(middle_kernel, nf, nt), out_shape=(jax.S...]
where the time goes in v3:
time: 198 us; the launch traced here: 197 us
  Pallas kernels  171 us (86%)
  matrix products  19.2 us (10%)
  local copies, waits for them, and re-layouts  4.74 us (2%)
    pallas_call x1, Pallas kernels, body(): pl.pallas_call(functools.partial(spread_kernel, nf, nt), out_shape=(jax.S...  76.8 us
    pallas_call x1, Pallas kernels, body(): pl.pallas_call(functools.partial(middle_kernel, nf, nt), out_shape=(jax.S...  65.6 us
    pallas_call x1, Pallas kernels, body(): pl.pallas_call(functools.partial(return_kernel, nf, nt), out_shape=jax.Sh...  28.8 us
    dot_general x1, matrix products, body(): lax.dot_general(whole, own[:, width:], contract, preferred_element_type=F32)  4.62 us

profile of v3, /device:TPU:13, one launch (start us, length us, event | category | flops | bytes accessed | tf_op | source)
XLA Modules:
  0.0 197.2 jit_solution(11430606227708740656)
XLA Ops:
  0.6 0.0 copy-start
  0.6 76.8 %spread.1 = (bf16[1024,2048]{1,0:T(8,128)(2,1)}, bf16[1024,2048]{1,0:T(8,128)(2,1)}) custom-call(bf16[256,1024]{1,0:T(8,128)(2,1)} %tokens.1, bf16[256,1024]{1,0:T(8,128)(2,1)} %grads.1), custom_call_target="tpu_custom_call" | custom-call | tf_op jit(solution)/shard_map/spread/pallas_call | solution.py:524
  77.5 1.1 constant_dynamic-update-slice_fusion.1
  78.6 0.0 copy-start.1
  78.7 1.3 constant_dynamic-update-slice_fusion.weights
  80.0 0.0 copy-start.3
  80.0 3.9 %fusion.4 = f32[1024,256]{1,0:T(8,128)S(1)} fusion(bf16[1024,2048]{1,0:T(8,128)(2,1)} %get-tuple-element.9, bf16[2048,256]{1,0:T(8,128)(2,1)S(1)} %constant_dynamic-update-slice_fusion.weights), kind=kOutput, calls=%fused_computation.11 | convolution fusion | flops 1073741824 | bytes 6291456 | tf_op jit(solution)/shard_map/dot_general | solution.py:547
  83.9 0.0 copy-done
  83.9 0.0 copy-done.1
  83.9 1.3 fusion.5
  85.2 0.0 copy-done.3
  85.2 1.3 pad_maximum_fusion.partial
  86.5 65.6 %middle.1 = (bf16[1024,2048]{1,0:T(8,128)(2,1)}, bf16[1024,128]{1,0:T(8,128)(2,1)}, bf16[256,2048]{1,0:T(8,128)(2,1)}) custom-call(f32[1024,384]{1,0:T(8,128)} %pad_maximum_fusion.partial, bf16[2048,256]{1,0:T(8,128)(2,1)} %copy-done.3), custom_call_target="tpu_custom_call" | custom-call | tf_op jit(solution)/shard_map/middle/pallas_call | solution.py:553
  152.1 0.0 copy-start.2
  152.1 4.6 %convolution_multiply_fusion.1 = f32[2048,128]{1,0:T(8,128)} fusion(bf16[1024,2048]{1,0:T(8,128)(2,1)} %get-tuple-element.9, bf16[1024,2048]{1,0:T(8,128)(2,1)} %get-tuple-element.11, s32[]{:T(128)S(6)} %add.4), kind=kOutput, calls=%fused_computation.1 | convolution fusion | flops 537133056 | bytes 5505028 | tf_op jit(solution)/shard_map/dot_general | solution.py:611
  156.7 0.0 copy-done.2
  156.7 0.0 copy-start.5
  156.7 0.0 copy-start.6
  156.7 3.4 %convolution_multiply_fusion.2 = f32[2048,128]{1,0:T(8,128)} fusion(bf16[1024,2048]{1,0:T(8,128)(2,1)S(1)} %copy-done.2, bf16[1024,2048]{1,0:T(8,128)(2,1)} %get-tuple-element.11, s32[]{:T(128)S(6)} %select_n.3), kind=kOutput, calls=%fused_computation.2 | convolution fusion | flops 537133056 | bytes 5505028 | tf_op jit(solution)/shard_map/dot_general | solution.py:608
  160.1 0.0 copy-done.5
  160.1 0.0 copy-done.6
  160.1 0.0 copy-start.4
  160.1 2.1 %convolution_convert_fusion.result = bf16[1024,256]{1,0:T(8,128)(2,1)} fusion(bf16[1024,2048]{1,0:T(8,128)(2,1)S(1)} %copy-done.5, bf16[256,2048]{1,0:T(8,128)(2,1)S(1)} %copy-done.6), kind=kOutput, calls=%fused_computation.4 | convolution fusion | flops 1074003968 | bytes 5767168 | tf_op jit(solution)/shard_map/dot_general | solution.py:585
  162.2 28.8 %back.1 = bf16[4,256,256]{2,1,0:T(8,128)(2,1)} custom-call(bf16[1024,256]{1,0:T(8,128)(2,1)} %convolution_convert_fusion.result), custom_call_target="tpu_custom_call" | custom-call | tf_op jit(solution)/shard_map/back/pallas_call | solution.py:588
  191.1 1.2 copy.13
  192.3 1.0 copy.14
  193.3 0.0 copy-done.4
  193.3 3.9 %convolution_multiply_fusion = f32[128,2048]{1,0:T(8,128)} fusion(bf16[1024,128]{1,0:T(8,128)(2,1)S(1)} %copy-done.4, bf16[1024,2048]{1,0:T(8,128)(2,1)} %get-tuple-element.10), kind=kOutput, calls=%fused_computation | convolution fusion | flops 537133056 | bytes 5505024 | tf_op jit(solution)/shard_map/dot_general | solution.py:614
Async XLA Ops:
  0.6 83.3 %copy-start = (bf16[128,2048]{1,0:T(8,128)(2,1)S(1)}, bf16[128,2048]{1,0:T(8,128)(2,1)}, u32[]{:S(2)}) copy-start(bf16[128,2048]{1,0:T(8,128)(2,1)} %param.9) | copy-start | bytes 1572868
  78.6 5.3 %copy-start.1 = (bf16[1024,2048]{1,0:T(8,128)(2,1)S(1)}, bf16[1024,2048]{1,0:T(8,128)(2,1)}, u32[]{:S(2)}) copy-start(bf16[1024,2048]{1,0:T(8,128)(2,1)} %get-tuple-element.10) | copy-start | bytes 12582916
  80.0 5.2 %copy-start.3 = (bf16[2048,256]{1,0:T(8,128)(2,1)}, bf16[2048,256]{1,0:T(8,128)(2,1)S(1)}, u32[]{:S(2)}) copy-start(bf16[2048,256]{1,0:T(8,128)(2,1)S(1)} %constant_dynamic-update-slice_fusion.weights) | copy-start | bytes 3145732
  152.1 4.6 %copy-start.2 = (bf16[1024,2048]{1,0:T(8,128)(2,1)S(1)}, bf16[1024,2048]{1,0:T(8,128)(2,1)}, u32[]{:S(2)}) copy-start(bf16[1024,2048]{1,0:T(8,128)(2,1)} %get-tuple-element.9) | copy-start | bytes 12582916
  156.7 3.4 %copy-start.5 = (bf16[1024,2048]{1,0:T(8,128)(2,1)S(1)}, bf16[1024,2048]{1,0:T(8,128)(2,1)}, u32[]{:S(2)}) copy-start(bf16[1024,2048]{1,0:T(8,128)(2,1)} %get-tuple-element.11) | copy-start | bytes 12582916
  156.7 3.4 %copy-start.6 = (bf16[256,2048]{1,0:T(8,128)(2,1)S(1)}, bf16[256,2048]{1,0:T(8,128)(2,1)}, u32[]{:S(2)}) copy-start(bf16[256,2048]{1,0:T(8,128)(2,1)} %get-tuple-element.12) | copy-start | bytes 3145732
  160.1 33.2 %copy-start.4 = (bf16[1024,128]{1,0:T(8,128)(2,1)S(1)}, bf16[1024,128]{1,0:T(8,128)(2,1)}, u32[]{:S(2)}) copy-start(bf16[1024,128]{1,0:T(8,128)(2,1)} %get-tuple-element.13) | copy-start | bytes 786436

commit v4 on v3

--- a/solution.py
+++ b/solution.py
@@ -14,6 +14,7 @@
 VMEM_LIMIT = 60 * 1024 * 1024
 CHUNKS = 4
 AHEAD = 2
+TILE = 512
 
 
 def place(nf, nt):
@@ -261,11 +262,19 @@
 def middle_kernel(
     nf,
     nt,
+    factor,
+    whole,
+    grads,
+    gate_weight,
+    up_weight,
+    down_weight,
+    all_out,
+    w_out,
+    gate_out,
+    up_out,
+    down_out,
     partial,
-    weights,
-    all_out,
     hidden_out,
-    w_out,
     landing,
     stage,
     hidden_own,
@@ -294,13 +303,31 @@
         return pl.ds(pl.multiple_of(g * rows, rows), rows)
 
     part = w_out.shape[0]
-    depth = weights.shape[1]
-    w_own = pltpu.make_async_copy(
-        weights.at[pl.ds(t * part, part)],
-        w_out.at[:, pl.ds(pl.multiple_of(t * depth, depth), depth)],
-        local_sem.at[1],
-    )
-    w_own.start()
+    ups = (gate_weight, up_weight)
+
+    def into(u, i):
+        return w_out.at[:, pl.ds(pl.multiple_of((2 * u + i) * width, width), width)]
+
+    def w_own(i):
+        return pltpu.make_async_copy(
+            ups[i].at[pl.ds(t * part, part)], into(t, i), local_sem.at[1 + i]
+        )
+
+    def multiply(g):
+        x = whole[block(g), :]
+        partial[block(g), :width] = jnp.dot(x, gate_weight[...], preferred_element_type=F32)
+        partial[block(g), width : 2 * width] = jnp.dot(
+            x, up_weight[...], preferred_element_type=F32
+        )
+        partial[block(g), 2 * width :] = lax.dot_general(
+            grads[block(g), :],
+            down_weight[...],
+            (((1,), (1,)), ((), ())),
+            preferred_element_type=F32,
+        )
+
+    for i in range(2):
+        w_own(i).start()
     enter(nf, nt)
 
     def share(g):
@@ -313,29 +340,27 @@
             partial.at[block(g)], landing.at[g], sum_send.at[g], sum_recv.at[g], (g, t)
         )
 
-    for j in range(1, nf):
-        share(lax.rem(f + j, nf)).start()
-
-    def w_copy(u):
-        return remote(
-            weights.at[pl.ds(u * part, part)],
-            w_out.at[:, pl.ds(pl.multiple_of(t * depth, depth), depth)],
-            w_send.at[u],
-            w_recv.at[t],
-            (f, u),
-        )
-
-    def w_in(u):
-        return remote(
-            weights.at[pl.ds(0, part)],
-            w_out.at[:, pl.ds(pl.multiple_of(u * depth, depth), depth)],
-            w_send.at[u],
-            w_recv.at[u],
-            (f, u),
+    def w_copy(u, i):
+        return remote(
+            ups[i].at[pl.ds(u * part, part)], into(t, i), w_send.at[u, i], w_recv.at[t, i], (f, u)
+        )
+
+    def w_in(u, i):
+        return remote(
+            ups[i].at[pl.ds(0, part)], into(u, i), w_send.at[u, i], w_recv.at[u, i], (f, u)
         )
 
     for j in range(1, nt):
-        w_copy(lax.rem(t + j, nt)).start()
+        for i in range(2):
+            w_copy(lax.rem(t + j, nt), i).start()
+
+    @pl.loop(1, nf + 1)
+    def _(j):
+        multiply(lax.rem(f + j, nf))
+
+        @pl.when(j > 1)
+        def _():
+            share(lax.rem(f + j - 1, nf)).start()
 
     for j in range(1, nf):
         share_in(lax.rem(f + j, nf)).wait_recv()
@@ -402,7 +427,7 @@
             here, here, pair_send.at[b, g], pair_recv.at[b, g], (f, t + 1 - 2 * k)
         )
 
-    for b in range(nz):
+    def pass_on(b):
         for j in range(nf):
             g = lax.rem(f + j, nf)
             if j == 0:
@@ -410,24 +435,50 @@
             else:
                 plane_in(b, g).wait_recv()
             pair(b, g).start()
+
+    h_keep.wait()
+    for j in range(1, nf):
+        h_in(lax.rem(f + j, nf)).wait_recv()
+    pass_on(z)
+    own = pl.ds(pl.multiple_of(t * 2 * width, 2 * width), 2 * width)
+    tile = min(TILE, whole.shape[1])
+    contract = (((0,), (0,)), ((), ()))
+
+    @pl.loop(0, whole.shape[1] // tile)
+    def _(i):
+        cols = pl.ds(pl.multiple_of(i * tile, tile), tile)
+        term = factor * lax.dot_general(
+            whole[:, cols], all_out[:, own], contract, preferred_element_type=F32
+        )
+        gate_out[cols, :] = term[:, :width]
+        up_out[cols, :] = term[:, width:]
+        down_out[:, cols] = factor * lax.dot_general(
+            hidden_out[...], grads[:, cols], contract, preferred_element_type=F32
+        )
+
+    for b in range(nz):
+
+        @pl.when(b != z)
+        def _(b=b):
+            pass_on(b)
+
     finish()
-    h_keep.wait()
     for j in range(1, nf):
         g = lax.rem(f + j, nf)
         share(g).wait_send()
         h_copy(g).wait_send()
-        h_in(g).wait_recv()
         for b in range(nz):
             plane(b, g).wait_send()
     for b in range(nz):
         for g in range(nf):
             pair(b, g).wait_send()
             pair_in(b, g).wait_recv()
-    w_own.wait()
-    for j in range(1, nt):
-        u = lax.rem(t + j, nt)
-        w_copy(u).wait_send()
-        w_in(u).wait_recv()
+    for i in range(2):
+        w_own(i).wait()
+        for j in range(1, nt):
+            u = lax.rem(t + j, nt)
+            w_copy(u, i).wait_send()
+            w_in(u, i).wait_recv()
 
 
 def return_kernel(nf, nt, result, out, landing, send, recv, send2, recv2, local_sem):
@@ -519,7 +570,6 @@
     factor = 1.0 / math.sqrt(count)
     assert nt == 2 * nf and depth == 2 * shard
 
-    pairs = jnp.concatenate([gate_weight, up_weight], axis=1)
     part = depth // nt
     whole, grads = pl.pallas_call(
         functools.partial(spread_kernel, nf, nt),
@@ -544,22 +594,20 @@
         name="spread",
     )(tokens, out_grad)
 
-    both = jnp.dot(whole, pairs, preferred_element_type=F32)
-    back = lax.dot_general(
-        grads, down_weight, (((1,), (1,)), ((), ())), preferred_element_type=F32
-    )
-    partial = jnp.concatenate([both, back], axis=1)
-
-    deltas, hidden, turned = pl.pallas_call(
-        functools.partial(middle_kernel, nf, nt),
+    deltas, turned, gate_grad, up_grad, down_grad = pl.pallas_call(
+        functools.partial(middle_kernel, nf, nt, factor),
         out_shape=(
             jax.ShapeDtypeStruct((count, nt * 2 * width), BF16),
-            jax.ShapeDtypeStruct((count, width), BF16),
             jax.ShapeDtypeStruct((part, nt * 2 * width), BF16),
+            jax.ShapeDtypeStruct((depth, width), F32),
+            jax.ShapeDtypeStruct((depth, width), F32),
+            jax.ShapeDtypeStruct((width, depth), F32),
         ),
-        in_specs=[VMEM, VMEM],
-        out_specs=(VMEM, VMEM, VMEM),
+        in_specs=[VMEM] * 5,
+        out_specs=(VMEM,) * 5,
         scratch_shapes=[
+            pltpu.VMEM((count, 3 * width), F32),
+            pltpu.VMEM((count, width), BF16),
             pltpu.VMEM((nf, rows, 3 * width), F32),
             pltpu.VMEM((1, nz, rows, 2 * width), BF16),
             pltpu.VMEM((rows, width), BF16),
@@ -574,13 +622,13 @@
             DMA((nz, nf)),
             DMA((nf,)),
             DMA((nf,)),
-            DMA((2,)),
-            DMA((nt,)),
-            DMA((nt,)),
+            DMA((3,)),
+            DMA((nt, 2)),
+            DMA((nt, 2)),
         ],
         compiler_params=params(1),
         name="middle",
-    )(partial, pairs)
+    )(whole, grads, gate_weight, up_weight, down_weight)
 
     piece = lax.dot_general(
         deltas, turned, (((1,), (1,)), ((), ())), preferred_element_type=F32
@@ -603,15 +651,6 @@
     )(piece)
     input_grad = input_grad.transpose(1, 0, 2).reshape(rows, shard)
 
-    own = lax.dynamic_slice_in_dim(deltas, lax.axis_index("tp") * 2 * width, 2 * width, 1)
-    contract = (((0,), (0,)), ((), ()))
-    gate_grad = factor * lax.dot_general(
-        whole, own[:, :width], contract, preferred_element_type=F32
-    )
-    up_grad = factor * lax.dot_general(
-        whole, own[:, width:], contract, preferred_element_type=F32
-    )
-    down_grad = factor * lax.dot_general(hidden, grads, contract, preferred_element_type=F32)
     return (input_grad, gate_grad, up_grad, down_grad)
 
 

time: 198 us -> 190 us (0.960)
  matrix products: 19.2 us -> 4.58 us
  Pallas kernels: 171 us -> 178 us
    dot_general x5 -> x0, matrix products: 17.1 us -> none  [the longest x1 4.62 us: body(): lax.dot_general(whole, own[:, width:], contract, preferred_element_type=F32)]
    pallas_call x1, Pallas kernels: 65.6 us -> 76.7 us  [body(): pl.pallas_call(functools.partial(middle_kernel, nf, nt, factor), out_shap...]
    pallas_call x1, Pallas kernels: 28.8 us -> 24.9 us  [body(): pl.pallas_call(functools.partial(return_kernel, nf, nt), out_shape=jax.Sh...]
    unnamed x16 -> x8, local copies, waits for them, and re-layouts: 2.17 us -> 5.21 us
    dot_general x1, matrix products: 2.09 us -> 4.58 us  [body(): lax.dot_general(deltas, turned, (((1,), (1,)), ((), ())), preferred_eleme...]
where the time goes in v4:
time: 190 us
  Pallas kernels  178 us (94%)
  local copies, waits for them, and re-layouts  6.46 us (3%)
  matrix products  4.58 us (2%)
    pallas_call x1, Pallas kernels, body(): pl.pallas_call(functools.partial(spread_kernel, nf, nt), out_shape=(jax.S...  76.8 us
    pallas_call x1, Pallas kernels, body(): pl.pallas_call(functools.partial(middle_kernel, nf, nt, factor), out_shap...  76.7 us
    pallas_call x1, Pallas kernels, body(): pl.pallas_call(functools.partial(return_kernel, nf, nt), out_shape=jax.Sh...  24.9 us
    unnamed x8, local copies, waits for them, and re-layouts  5.21 us
    dot_general x1, matrix products, body(): lax.dot_general(deltas, turned, (((1,), (1,)), ((), ())), preferred_eleme...  4.58 us

profile of v4, /device:TPU:13, one launch (start us, length us, event | category | flops | bytes accessed | tf_op | source)
XLA Modules:
  0.0 190.2 jit_solution(9367059083281467404)
XLA Ops:
  0.6 76.8 %spread.1 = (bf16[1024,2048]{1,0:T(8,128)(2,1)}, bf16[1024,2048]{1,0:T(8,128)(2,1)}) custom-call(bf16[256,1024]{1,0:T(8,128)(2,1)} %tokens.1, bf16[256,1024]{1,0:T(8,128)(2,1)} %grads.1), custom_call_target="tpu_custom_call" | custom-call | tf_op jit(solution)/shard_map/spread/pallas_call | solution.py:574
  77.5 76.7 %middle.1 = (bf16[1024,2048]{1,0:T(8,128)(2,1)}, bf16[256,2048]{1,0:T(8,128)(2,1)}, f32[2048,128]{1,0:T(8,128)}, f32[2048,128]{1,0:T(8,128)}, f32[128,2048]{1,0:T(8,128)}) custom-call(bf16[1024,2048]{1,0:T(8,128)(2,1)} %get-tuple-element.11.whole, bf16[1024,2048]{1,0:T(8,128)(2,1)} %get-tuple-element.12.grads, bf16[2048,128]{1,0:T(8,128)(2,1)} %gate_weight.1, ...), custom_call_target="tpu_custom_call" | custom-call | tf_op jit(solution)/shard_map/middle/pallas_call | solution.py:597
  154.2 4.6 %convolution_convert_fusion.result = bf16[1024,256]{1,0:T(8,128)(2,1)} fusion(bf16[1024,2048]{1,0:T(8,128)(2,1)} %get-tuple-element.13, bf16[256,2048]{1,0:T(8,128)(2,1)} %get-tuple-element.14), kind=kOutput, calls=%fused_computation | convolution fusion | flops 1074003968 | bytes 5767168 | tf_op jit(solution)/shard_map/dot_general | solution.py:633
  158.8 0.0 copy-start.1
  158.8 0.0 copy-start
  158.8 24.9 %back.1 = bf16[4,256,256]{2,1,0:T(8,128)(2,1)} custom-call(bf16[1024,256]{1,0:T(8,128)(2,1)} %convolution_convert_fusion.result), custom_call_target="tpu_custom_call" | custom-call | tf_op jit(solution)/shard_map/back/pallas_call | solution.py:636
  183.7 1.2 copy.9
  185.0 1.0 copy.10
  186.0 2.3 %copy.14 = f32[2048,128]{1,0:T(8,128)} copy(f32[2048,128]{1,0:T(8,128)} %get-tuple-element.27) | data formatting | bytes 2097152
  188.2 0.0 copy-done.1
  188.2 1.0 copy.15
  189.2 0.0 copy-done
  189.2 1.0 copy.16
Async XLA Ops:
  158.8 29.5 %copy-start.1 = (f32[2048,128]{1,0:T(8,128)S(1)}, f32[2048,128]{1,0:T(8,128)}, u32[]{:S(2)}) copy-start(f32[2048,128]{1,0:T(8,128)} %get-tuple-element.28) | copy-start | bytes 3145732
  158.8 30.4 %copy-start = (f32[128,2048]{1,0:T(8,128)S(1)}, f32[128,2048]{1,0:T(8,128)}, u32[]{:S(2)}) copy-start(f32[128,2048]{1,0:T(8,128)} %get-tuple-element.29) | copy-start | bytes 3145732

commit v5 on v4

--- a/solution.py
+++ b/solution.py
@@ -481,7 +481,7 @@
             w_in(u, i).wait_recv()
 
 
-def return_kernel(nf, nt, result, out, landing, send, recv, send2, recv2, local_sem):
+def return_kernel(nf, nt, deltas, turned, out, result, landing, send, recv, send2, recv2, local_sem):
     f, t = place(nf, nt)
     rows = landing.shape[1]
 
@@ -489,7 +489,6 @@
         return pl.ds(pl.multiple_of(g * rows, rows), rows)
 
     keep = pltpu.make_async_copy(result.at[block(f)], landing.at[f], local_sem.at[0])
-    keep.start()
     enter(nf, nt)
 
     def first(g):
@@ -498,8 +497,21 @@
     def first_in(g):
         return remote(result.at[block(g)], landing.at[g], send.at[g], recv.at[g], (g, t))
 
-    for j in range(1, nf):
-        first(lax.rem(f + j, nf)).start()
+    @pl.loop(1, nf + 1)
+    def _(j):
+        g = lax.rem(f + j, nf)
+        result[block(g), :] = lax.dot_general(
+            deltas[block(g), :],
+            turned[...],
+            (((1,), (1,)), ((), ())),
+            preferred_element_type=F32,
+        ).astype(BF16)
+
+        @pl.when(j > 1)
+        def _():
+            first(lax.rem(f + j - 1, nf)).start()
+
+    keep.start()
     keep.wait()
     lane = lax.rem(t, nf)
 
@@ -630,15 +642,13 @@
         name="middle",
     )(whole, grads, gate_weight, up_weight, down_weight)
 
-    piece = lax.dot_general(
-        deltas, turned, (((1,), (1,)), ((), ())), preferred_element_type=F32
-    ).astype(BF16)
     input_grad = pl.pallas_call(
         functools.partial(return_kernel, nf, nt),
         out_shape=jax.ShapeDtypeStruct((nf, rows, part), BF16),
-        in_specs=[VMEM],
+        in_specs=[VMEM, VMEM],
         out_specs=VMEM,
         scratch_shapes=[
+            pltpu.VMEM((count, part), BF16),
             pltpu.VMEM((nf, rows, part), BF16),
             DMA((nf,)),
             DMA((nf,)),
@@ -648,7 +658,7 @@
         ],
         compiler_params=params(2),
         name="back",
-    )(piece)
+    )(deltas, turned)
     input_grad = input_grad.transpose(1, 0, 2).reshape(rows, shard)
 
     return (input_grad, gate_grad, up_grad, down_grad)

time: 190 us -> 188 us (0.989)
  matrix products: 4.58 us -> 0 us
  Pallas kernels: 178 us -> 181 us
    dot_general x1 -> x0, matrix products: 4.58 us -> none  [body(): lax.dot_general(deltas, turned, (((1,), (1,)), ((), ())), preferred_eleme...]
    pallas_call x1, Pallas kernels: 24.9 us -> 27.1 us  [body(): pl.pallas_call(functools.partial(return_kernel, nf, nt), out_shape=jax.Sh...]
where the time goes in v5:
time: 188 us
  Pallas kernels  181 us (96%)
  local copies, waits for them, and re-layouts  6.54 us (3%)
    pallas_call x1, Pallas kernels, body(): pl.pallas_call(functools.partial(spread_kernel, nf, nt), out_shape=(jax.S...  76.9 us
    pallas_call x1, Pallas kernels, body(): pl.pallas_call(functools.partial(middle_kernel, nf, nt, factor), out_shap...  76.7 us
    pallas_call x1, Pallas kernels, body(): pl.pallas_call(functools.partial(return_kernel, nf, nt), out_shape=jax.Sh...  27.1 us
    unnamed x8, local copies, waits for them, and re-layouts  5.21 us

profile of v5, /device:TPU:13, one launch (start us, length us, event | category | flops | bytes accessed | tf_op | source)
XLA Modules:
  0.0 187.9 jit_solution(10573618066742863600)
XLA Ops:
  0.6 76.9 %spread.1 = (bf16[1024,2048]{1,0:T(8,128)(2,1)}, bf16[1024,2048]{1,0:T(8,128)(2,1)}) custom-call(bf16[256,1024]{1,0:T(8,128)(2,1)} %tokens.1, bf16[256,1024]{1,0:T(8,128)(2,1)} %grads.1), custom_call_target="tpu_custom_call" | custom-call | tf_op jit(solution)/shard_map/spread/pallas_call | solution.py:586
  77.5 76.7 %middle.1 = (bf16[1024,2048]{1,0:T(8,128)(2,1)}, bf16[256,2048]{1,0:T(8,128)(2,1)}, f32[2048,128]{1,0:T(8,128)}, f32[2048,128]{1,0:T(8,128)}, f32[128,2048]{1,0:T(8,128)}) custom-call(bf16[1024,2048]{1,0:T(8,128)(2,1)} %get-tuple-element.11.whole, bf16[1024,2048]{1,0:T(8,128)(2,1)} %get-tuple-element.12.grads, bf16[2048,128]{1,0:T(8,128)(2,1)} %gate_weight.1, ...), custom_call_target="tpu_custom_call" | custom-call | tf_op jit(solution)/shard_map/middle/pallas_call | solution.py:609
  154.2 0.0 copy-start.1
  154.2 27.1 %back.1 = bf16[4,256,256]{2,1,0:T(8,128)(2,1)} custom-call(bf16[1024,2048]{1,0:T(8,128)(2,1)} %get-tuple-element.13.deltas, bf16[256,2048]{1,0:T(8,128)(2,1)} %get-tuple-element.14.turned), custom_call_target="tpu_custom_call" | custom-call | tf_op jit(solution)/shard_map/back/pallas_call | solution.py:645
  181.3 0.0 copy-start
  181.4 1.3 copy.9
  182.7 1.0 copy.10
  183.7 2.3 %copy.14 = f32[2048,128]{1,0:T(8,128)} copy(f32[2048,128]{1,0:T(8,128)} %get-tuple-element.27) | data formatting | bytes 2097152
  186.0 0.0 copy-done.1
  186.0 1.0 copy.15
  186.9 0.0 copy-done
  186.9 1.0 copy.16
Async XLA Ops:
  154.2 31.8 %copy-start.1 = (f32[2048,128]{1,0:T(8,128)S(1)}, f32[2048,128]{1,0:T(8,128)}, u32[]{:S(2)}) copy-start(f32[2048,128]{1,0:T(8,128)} %get-tuple-element.28) | copy-start | bytes 3145732
  181.3 5.6 %copy-start = (f32[128,2048]{1,0:T(8,128)S(1)}, f32[128,2048]{1,0:T(8,128)}, u32[]{:S(2)}) copy-start(f32[128,2048]{1,0:T(8,128)} %get-tuple-element.29) | copy-start | bytes 3145732
